TPU v7x, 256 devices: a 2x2x32 block of a 4x8x32 slice. The times are simulated.
256 devices in a mesh: groups: 4 (over y, x), asset: 64 (over z, core).
Axes of the slice: x: 2, y: 2, z: 32, core: 2. Of those that a mesh axis runs over, the one named last changes fastest.
The devices are a block of a 4x8x32 slice.
Arguments:
- scen_draws: bfloat16 [16384, 256], P(('groups', 'asset')), parts along dimension 0, may hold values from -4 to 4
- factor_mix: bfloat16 [256, 256], replicated, may hold values from -0.375 to 0.375
- loadings: bfloat16 [262144, 256], P(('groups', 'asset')), parts along dimension 0, may hold values from -0.375 to 0.375
- convexity: float32 [262144], P(('groups', 'asset')), parts along dimension 0, may hold values from -0.6 to 0.6
- holdings: float32 [262144], P(('groups', 'asset')), parts along dimension 0, may hold values from -0.110485435 to 0.110485435
- desk_map: int32 [262144], P(('groups', 'asset')), parts along dimension 0, may hold values from 0 to 127
- ranks: int32 [16384], P('groups'), parts along dimension 0, may hold values from 0 to 4095, each once
- desk_prices: float32 [512], P('groups'), parts along dimension 0, may hold values from -5 to 5
Outputs:
- allocation: float32 [512], P('groups'), parts along dimension 0
- grad_loadings: float32 [262144, 256], P(('groups', 'asset')), parts along dimension 0
- grad_convexity: float32 [262144], P(('groups', 'asset')), parts along dimension 0
There are 4 independent parts, one for each index of `groups`. A program takes and returns all parts, laid end to end along the dimension named above; an argument that names none is the same for every part. Nothing has to cross between parts.
All inputs are finite; a program needn't handle non-finite values.
Results may differ from a plain program's by a relative error of at most 0.0029.
Values may be sent and summed in bfloat16 or wider, within the bound.
No kernel may reach another device: no remote copies, remote signals or barrier semaphores. Data moves between devices by JAX's collectives and lax.ppermute only.
A program may use at most 64 MiB of HBM per device.

v0:
```python
import math
import jax
import jax.numpy as jnp
from jax import lax
from jax.sharding import Mesh
from jax.sharding import PartitionSpec as P

DESKS = 128
BAND = 32
CENTER = 166
ASSET = ("asset_0", "asset_1")
GROUPS_ASSET = ("groups", "asset_0", "asset_1")


def filled_up(lines, size):
    spare = -lines.shape[0] % size
    if not spare:
        return lines
    return jnp.concatenate([lines, jnp.zeros((spare, *lines.shape[1:]), lines.dtype)])


def copy_for_each(x, axis):
    copies = jnp.broadcast_to(x, (lax.axis_size(axis), *x.shape))
    return lax.all_to_all(copies, axis, split_axis=0, concat_axis=0, tiled=True)


def laid_out(tiles, dim):
    tiles = jnp.moveaxis(tiles, 0, dim)
    shape = tiles.shape
    return tiles.reshape(*shape[:dim], shape[dim] * shape[dim + 1], *shape[dim + 2 :])


def collect(x, axis, dim):
    tiles = copy_for_each(x, axis)
    return laid_out(tiles, dim)


def cut_along(x, dim, size):
    before, after = (x.shape[:dim], x.shape[dim + 1 :])
    return jnp.moveaxis(x.reshape(*before, size, -1, *after), dim, 0)


def summed_on_arrival(x, axis, dim):
    size = lax.axis_size(axis)
    tiles = lax.all_to_all(cut_along(x, dim, size), axis, 0, 0, tiled=True)
    return jnp.sum(tiles, axis=0)


def total_of(x, axes):
    padded = filled_up(x, lax.axis_size(axes))
    whole = collect(summed_on_arrival(padded, axes, 0), axes, 0)
    return lax.slice_in_dim(whole, 0, len(x)).reshape(x.shape)


def packed_total(arrays, axis):
    ends = [0]
    for a in arrays:
        ends.append(ends[-1] + a.size)
    running = total_of(jnp.concatenate([a.ravel() for a in arrays]), axis)
    return tuple((running[b:e].reshape(a.shape) for a, b, e in zip(arrays, ends, ends[1:])))


def over_axes(x, axes):
    for axis in axes:
        x = lax.psum(x, axis)
    return x


def gather_axes(x, axes, dim):
    far, near = axes
    first = copy_for_each(x, far)
    tiles = jnp.swapaxes(copy_for_each(first, near), 0, 1)
    return laid_out(tiles.reshape(-1, *x.shape), dim)


def smooth_bend(value):
    return jnp.logaddexp(value, -value) - math.log(2.0)


def rank_kernel(ranks, scenarios):
    centre = jnp.float32(CENTER)
    spread = jnp.float32(BAND)
    offsets = (ranks.astype(jnp.float32) - centre) / spread
    every = (jnp.arange(scenarios, dtype=jnp.float32) - centre) / spread
    return jnp.exp(-0.5 * offsets * offsets) / jnp.sum(jnp.exp(-0.5 * every * every))


def cotangent_of(
    weights,
    weight_total,
    slopes,
    smoothing,
    kernel,
    grad_quant,
    grad_band,
    centred,
    prices,
    scenarios,
):
    grad_loss = (
        slopes / smoothing
        + kernel * grad_quant
        + grad_band * 0.09 * centred / (scenarios * smoothing)
    )
    return (
        scenarios * (-weights[:, None] * prices[None, :] / weight_total - grad_loss[:, None])
    ).astype(jnp.bfloat16)


def tail_core(losses, valued, ranks, prices):
    scenarios = losses.shape[0]
    kernel = rank_kernel(ranks, scenarios)
    quantile = jnp.sum(kernel * losses)
    average = jnp.mean(losses)
    centred = losses - average
    smoothing = 0.3 * jnp.sqrt(jnp.mean(centred * centred) + 1e-06)
    scores = (losses - quantile) / smoothing
    weights = jax.nn.sigmoid(scores)
    weight_total = jnp.sum(weights)
    objective = -jnp.sum(weights * valued) / weight_total
    slopes = (-valued - objective) / weight_total * weights * (1.0 - weights)
    grad_quant = -jnp.sum(slopes) / smoothing
    grad_band = -jnp.sum(slopes * scores) / smoothing
    cotangent = cotangent_of(
        weights,
        weight_total,
        slopes,
        smoothing,
        kernel,
        grad_quant,
        grad_band,
        centred,
        prices,
        scenarios,
    )
    return (cotangent, weights, weight_total)


def tail_columns(partial_value, ranks, prices):
    sums = packed_total(
        (-jnp.sum(partial_value, axis=1), jnp.sum(partial_value * prices[None, :], axis=1)), ASSET
    )
    cotangent, weights, weight_total = tail_core(sums[0], sums[1], ranks, prices)
    weighted = over_axes(jnp.sum(weights[:, None] * partial_value, axis=0), ASSET)
    return (cotangent, -weighted / weight_total)


def desk_table(desk_map):
    columns = jnp.arange(DESKS, dtype=jnp.int32)
    return (desk_map[:, None] == columns[None, :]).astype(jnp.bfloat16)


def split_rows(array, block_rows):
    return array.reshape((-1, block_rows) + array.shape[1:])


def exposure_of(shock_rows, loadings):
    return lax.dot_general(
        shock_rows, loadings, (((1,), (1,)), ((), ())), preferred_element_type=jnp.float32
    )


def pnl_rows(shock_rows, loadings, convexity, holdings, table):
    number = shock_rows.shape[0]
    block_rows = math.gcd(number, 512)

    def pnl_one_block(shock_block):
        exposure = exposure_of(shock_block, loadings)
        held = (holdings * (exposure + convexity * smooth_bend(exposure))).astype(jnp.bfloat16)
        return jnp.dot(held, table, preferred_element_type=jnp.float32)

    result = lax.map(pnl_one_block, split_rows(shock_rows, block_rows))
    return result.reshape((number, table.shape[1]))


def grad_rows(carry, shock_rows, cot_rows, loadings, convexity, holdings, table):
    number = shock_rows.shape[0]
    block_rows = math.gcd(number, 512)

    def grad_one_block(state, inputs):
        shock_block, cot_block = inputs
        exposure = exposure_of(shock_block, loadings)
        spread_back = lax.dot_general(
            cot_block, table, (((1,), (1,)), ((), ())), preferred_element_type=jnp.float32
        )
        held = holdings * spread_back
        grad_exposure = (held * (1.0 + convexity * jnp.tanh(exposure))).astype(jnp.bfloat16)
        grad_load = state[0] + lax.dot_general(
            grad_exposure, shock_block, (((0,), (0,)), ((), ())), preferred_element_type=jnp.float32
        )
        grad_conv = state[1] + jnp.sum(held * smooth_bend(exposure), axis=0)
        return ((grad_load, grad_conv), None)

    final, ignored = lax.scan(
        grad_one_block,
        carry,
        (split_rows(shock_rows, block_rows), split_rows(cot_rows, block_rows)),
    )
    return final


def shards(scen_draws, factor_mix, loadings, convexity, holdings, desk_map, ranks, desk_prices):
    local_shocks = jnp.dot(scen_draws, factor_mix, preferred_element_type=jnp.float32).astype(
        jnp.bfloat16
    )
    table = desk_table(desk_map)
    shocks = gather_axes(local_shocks, ("asset_0", "asset_1"), 0)
    partial_value = pnl_rows(shocks, loadings, convexity, holdings, table)
    cotangent, allocation = tail_columns(partial_value, ranks, desk_prices)
    initial = (
        jnp.zeros((loadings.shape[0], loadings.shape[1]), jnp.float32),
        jnp.zeros((loadings.shape[0],), jnp.float32),
    )
    grad_load, grad_conv = grad_rows(
        initial, shocks, cotangent, loadings, convexity, holdings, table
    )
    squares = over_axes(jnp.sum(grad_load * grad_load) + jnp.sum(grad_conv * grad_conv), ASSET)
    entries = loadings.shape[0] * lax.axis_size(ASSET) * (loadings.shape[1] + 1)
    factor = lax.rsqrt(squares / entries + 1e-06)
    return (allocation, grad_load * factor, grad_conv * factor)


def solution(mesh):
    torus = Mesh(
        mesh.devices.reshape(mesh.shape["groups"], 32, 2), ("groups", "asset_0", "asset_1")
    )
    return jax.shard_map(
        shards,
        mesh=torus,
        in_specs=(
            P(GROUPS_ASSET, None),
            P(),
            P(GROUPS_ASSET, None),
            P(GROUPS_ASSET),
            P(GROUPS_ASSET),
            P(GROUPS_ASSET),
            P("groups"),
            P("groups"),
        ),
        out_specs=(P("groups"), P(GROUPS_ASSET, None), P(GROUPS_ASSET)),
        check_vma=False,
    )
```

profile of v0, /device:TPU:37, one launch (start us, length us, event | category | flops | bytes accessed | tf_op | source)
XLA Modules:
  0.0 359.4 jit_solution(15060804531510212304)
XLA Ops:
  3.5 33.2 %all-to-all-start = ((bf16[32,64,256]{2,1,0:T(8,128)(2,1)}), bf16[32,64,256]{2,1,0:T(8,128)(2,1)S(1)}, u32[]{:S(2)}, u32[]{:S(2)}) async-start(bf16[32,64,256]{2,1,0:T(8,128)(2,1)} %broadcast_in_dim.37), calls=%async_computation | async-start | bytes 2097152 | tf_op jit(solution)/shard_map/all_to_all | solution.py:24
  36.8 104.4 %all-to-all-done = bf16[32,64,256]{2,1,0:T(8,128)(2,1)S(1)} async-done(((bf16[32,64,256]{2,1,0:T(8,128)(2,1)}), bf16[32,64,256]{2,1,0:T(8,128)(2,1)S(1)}, u32[]{:S(2)}, u32[]{:S(2)}) %all-to-all-start) | async-done | bytes 1048608 | tf_op jit(solution)/shard_map/all_to_all | solution.py:24
  141.4 6.0 %all_to_all.25 = bf16[2,32,64,256]{3,2,1,0:T(8,128)(2,1)S(1)} all-to-all(bf16[2,32,64,256]{3,2,1,0:T(8,128)(2,1)S(1)} %broadcast_in_dim.38), channel_id=1, replica_groups=mesh['groups'=4,'asset_0'=32,'asset_1'=2] {'asset_1'}, dimensions={0} | all-to-all | bytes 4194304 | tf_op jit(solution)/shard_map/all_to_all | solution.py:24
  149.0 23.4 %while.28 = (s32[]{:T(128)}, f32[8,512,128]{2,1,0:T(8,128)S(1)}, f32[1024]{0:T(1024)S(1)}, bf16[8,512,256]{2,1,0:T(8,128)(2,1)}, bf16[1024,256]{1,0:T(8,128)(2,1...) while((s32[]{:T(128)}, f32[8,512,128]{2,1,0:T(8,128)S(1)}, f32[1024]{0:T(1024)S(1)}, ...), condition=%wide.region_1.2_spmd.clone, body=%wide.region_0.1_spmd.clone.sunk | while | flops 410255360 | bytes 1061981 | solution.py:172
  149.0 2.9 fusion.83
  151.9 2.9 fusion.83
  154.8 2.9 fusion.83
  157.7 2.9 fusion.83
  160.7 2.9 fusion.83
  163.6 2.9 fusion.83
  166.5 2.9 fusion.83
  169.4 2.9 fusion.83
  173.6 30.4 %all_to_all.26 = f32[64,1,128]{2,1,0:T(1,128)S(1)} all-to-all(f32[64,1,128]{2,1,0:T(1,128)S(1)} %bitcast.91), channel_id=1, replica_groups=mesh['groups'=4,'asset_0'=32,'asset_1'=2] {'asset_0','asset_1'}, dimensions={0} | all-to-all | bytes 65536 | tf_op jit(solution)/shard_map/all_to_all | solution.py:45
  204.7 6.3 %all-to-all-start.3 = ((f32[64,1,128]{2,1,0:T(1,128)}), f32[64,1,128]{2,1,0:T(1,128)S(1)}, u32[]{:S(2)}, u32[]{:S(2)}) async-start(f32[64,1,128]{2,1,0:T(1,128)} %broadcast_in_dim.39), calls=%async_computation.3 | async-start | bytes 65536 | tf_op jit(solution)/shard_map/all_to_all | solution.py:24
  211.6 22.0 %all-to-all-done.3 = f32[64,1,128]{2,1,0:T(1,128)S(1)} async-done(((f32[64,1,128]{2,1,0:T(1,128)}), f32[64,1,128]{2,1,0:T(1,128)S(1)}, u32[]{:S(2)}, u32[]{:S(2)}) %all-to-all-start.3) | async-done | bytes 32800 | tf_op jit(solution)/shard_map/all_to_all | solution.py:24
  248.6 47.0 %while.29 = (s32[]{:T(128)}, f32[1024,256]{1,0:T(8,128)S(1)}, f32[1024]{0:T(1024)S(1)}, f32[1024]{0:T(1024)S(1)}, bf16[8,512,128]{2,1,0:T(8,128)(2,1)S(1)}, /*in...) while((s32[]{:T(128)}, f32[1024,256]{1,0:T(8,128)S(1)}, ...), condition=%wide.region_18.19_spmd.clone, body=%wide.region_16.18_spmd.clone.sunk | while | flops 681313280 | bytes 15892648 | solution.py:194
  249.6 2.8 fusion.89
  255.5 2.8 fusion.89
  258.3 2.0 convolution_add_fusion.2
  261.4 2.8 fusion.89
  264.2 2.0 convolution_add_fusion.2
  267.3 2.8 fusion.89
  270.0 2.0 convolution_add_fusion.2
  273.2 2.8 fusion.89
  275.9 2.0 convolution_add_fusion.2
  279.0 2.8 fusion.89
  281.8 2.0 convolution_add_fusion.2
  284.9 2.8 fusion.89
  287.7 2.0 convolution_add_fusion.2
  290.8 2.8 fusion.89
  298.4 40.2 %all-reduce = (f32[128]{0:T(128)S(1)}, f32[]{:T(128)}) all-reduce(f32[128]{0:T(128)S(1)} %multiply_reduce_fusion, f32[]{:T(128)S(6)} %add.117), channel_id=1, replica_groups=mesh['groups'=4,'asset_0'=32,'asset_1'=2] {'asset_0'}, use_global_device_ids=true, to_apply=%region_10.11 | all-reduce | flops 129 | bytes 1032 | tf_op jit(solution)/shard_map/psum | solution.py:65
  338.6 17.4 %all-reduce.1 = (f32[128]{0:T(128)S(1)}, f32[]{:T(128)}) all-reduce(f32[128]{0:T(128)S(1)} %get-tuple-element.297, f32[]{:T(128)} %get-tuple-element.298), channel_id=1, replica_groups=mesh['groups'=4,'asset_0'=32,'asset_1'=2] {'asset_1'}, use_global_device_ids=true, to_apply=%region_11.12 | all-reduce | flops 129 | bytes 1032 | tf_op jit(solution)/shard_map/psum | solution.py:65
  (82 shorter events, 34.6 us)
Async XLA Ops:
  0.6 0.9 copy-start
  3.5 137.7 %all-to-all-start = ((bf16[32,64,256]{2,1,0:T(8,128)(2,1)}), bf16[32,64,256]{2,1,0:T(8,128)(2,1)S(1)}, u32[]{:S(2)}, u32[]{:S(2)}) async-start(bf16[32,64,256]{2,1,0:T(8,128)(2,1)} %broadcast_in_dim.37), calls=%async_computation | async-start | bytes 2097152 | tf_op jit(solution)/shard_map/all_to_all | solution.py:24
  147.4 1.5 copy-start.1
  147.4 1.5 copy-start.2
  147.4 1.5 copy-start.3
  147.4 1.5 copy-start.6
  148.9 23.4 %copy-start.5 = (f32[128]{0:T(128)S(1)}, f32[128]{0:T(128)}, u32[]{:S(2)}) copy-start(f32[128]{0:T(128)} %param.19) | copy-start | bytes 1540
  172.4 63.9 %copy-start.4 = (s32[4096]{0:T(1024)S(1)}, s32[4096]{0:T(1024)}, u32[]{:S(2)}) copy-start(s32[4096]{0:T(1024)} %param.18) | copy-start | bytes 49156
  204.7 28.9 %all-to-all-start.3 = ((f32[64,1,128]{2,1,0:T(1,128)}), f32[64,1,128]{2,1,0:T(1,128)S(1)}, u32[]{:S(2)}, u32[]{:S(2)}) async-start(f32[64,1,128]{2,1,0:T(1,128)} %broadcast_in_dim.39), calls=%async_computation.3 | async-start | bytes 65536 | tf_op jit(solution)/shard_map/all_to_all | solution.py:24
  248.6 1.0 copy-start.7
  254.5 1.0 copy-start.7
  260.4 1.0 copy-start.7
  266.2 1.0 copy-start.7
  272.1 1.0 copy-start.7
  278.0 1.0 copy-start.7
  283.9 1.0 copy-start.7
  289.7 1.0 copy-start.7
where the time goes:
time: 361 us; the launch traced here: 359 us
  waiting for transfers between devices  126 us (35%)
  blocking collectives  94 us (26%)
  matrix products  66.8 us (19%)
  starting transfers between devices  39.5 us (11%)
  other arithmetic  17 us (5%)
  local copies, waits for them, and re-layouts  8.24 us (2%)
  between operations  6.85 us (2%)
    all_to_all x2, waiting for transfers between devices, copy_for_each(): return lax.all_to_all(copies, axis, split_axis=0, concat_axis=0, tiled=True)  126 us
    psum x2, blocking collectives, over_axes(): x = lax.psum(x, axis)  57.6 us
    all_to_all x2, starting transfers between devices, copy_for_each(): return lax.all_to_all(copies, axis, split_axis=0, concat_axis=0, tiled=True)  39.5 us
    all_to_all x1, blocking collectives, summed_on_arrival(): tiles = lax.all_to_all(cut_along(x, dim, size), axis, 0, 0, tiled=True)  30.4 us
    dot_general x8, matrix products, pnl_one_block(): return jnp.dot(held, table, preferred_element_type=jnp.float32)  23.2 us
    dot_general x8, matrix products, exposure_of(): lax.dot_general(shock_rows, loadings, (((1,), (1,)), ((), ())), preferred...  22.1 us
    dot_general x8, matrix products, grad_one_block(): lax.dot_general(grad_exposure, shock_block, (((0,), (0,)), ((), ())), pre...  16.3 us
  transfers between devices with their start and end apart: 2, of which 2 were waited for; matrix products, arithmetic and copies ran while one was open for 0% of the time, Pallas kernels for 0%

commit v1 on v0

--- a/solution.py
+++ b/solution.py
@@ -62,7 +62,8 @@
 
 def over_axes(x, axes):
     for axis in axes:
-        x = lax.psum(x, axis)
+        blocks = lax.all_gather(x, axis, axis=0, tiled=False)
+        x = blocks.sum(axis=0)
     return x
 
 

time: 361 us -> 438 us (1.21)
  blocking collectives: 94 us -> 147 us
  matrix products: 66.8 us -> 89.3 us
    psum x2 -> x0, blocking collectives: 57.6 us -> none  [over_axes(): x = lax.psum(x, axis)]
    unnamed x0 -> x2, blocking collectives: none -> 56.5 us
    all_gather x0 -> x2, blocking collectives: none -> 54.5 us  [over_axes(): blocks = lax.all_gather(x, axis, axis=0, tiled=False)]
    dot_general x8, matrix products: 22.1 us -> 32 us  [exposure_of(): lax.dot_general(shock_rows, loadings, (((1,), (1,)), ((), ())), preferred...]
    dot_general x8, matrix products: 4.4 us -> 12.1 us  [grad_one_block(): lax.dot_general(cot_block, table, (((1,), (1,)), ((), ())), preferred_ele...]
    dot_general x8, matrix products: 16.3 us -> 21.1 us  [grad_one_block(): lax.dot_general(grad_exposure, shock_block, (((0,), (0,)), ((), ())), pre...]
where the time goes in v1:
time: 438 us; the launch traced here: 437 us
  blocking collectives  147 us (34%)
  waiting for transfers between devices  125 us (29%)
  matrix products  89.3 us (20%)
  starting transfers between devices  39.5 us (9%)
  other arithmetic  20.1 us (5%)
  local copies, waits for them, and re-layouts  7.89 us (2%)
  between operations  6.86 us (2%)
    all_to_all x2, waiting for transfers between devices, copy_for_each(): return lax.all_to_all(copies, axis, split_axis=0, concat_axis=0, tiled=True)  125 us
    unnamed x2, blocking collectives  56.5 us
    all_gather x2, blocking collectives, over_axes(): blocks = lax.all_gather(x, axis, axis=0, tiled=False)  54.5 us
    all_to_all x2, starting transfers between devices, copy_for_each(): return lax.all_to_all(copies, axis, split_axis=0, concat_axis=0, tiled=True)  39.5 us
    dot_general x8, matrix products, exposure_of(): lax.dot_general(shock_rows, loadings, (((1,), (1,)), ((), ())), preferred...  32 us
    all_to_all x1, blocking collectives, summed_on_arrival(): tiles = lax.all_to_all(cut_along(x, dim, size), axis, 0, 0, tiled=True)  30.4 us
    dot_general x8, matrix products, pnl_one_block(): return jnp.dot(held, table, preferred_element_type=jnp.float32)  23.1 us
    dot_general x8, matrix products, grad_one_block(): lax.dot_general(grad_exposure, shock_block, (((0,), (0,)), ((), ())), pre...  21.1 us
  transfers between devices with their start and end apart: 2, of which 2 were waited for; matrix products, arithmetic and copies ran while one was open for 0% of the time, Pallas kernels for 0%

profile of v1, /device:TPU:37, one launch (start us, length us, event | category | flops | bytes accessed | tf_op | source)
XLA Modules:
  0.0 436.7 jit_solution(2688008372581270954)
XLA Ops:
  3.5 33.2 %all-to-all-start = ((bf16[32,64,256]{2,1,0:T(8,128)(2,1)}), bf16[32,64,256]{2,1,0:T(8,128)(2,1)S(1)}, u32[]{:S(2)}, u32[]{:S(2)}) async-start(bf16[32,64,256]{2,1,0:T(8,128)(2,1)} %broadcast_in_dim.37), calls=%async_computation | async-start | bytes 2097152 | tf_op jit(solution)/shard_map/all_to_all | solution.py:24
  36.8 104.4 %all-to-all-done = bf16[32,64,256]{2,1,0:T(8,128)(2,1)S(1)} async-done(((bf16[32,64,256]{2,1,0:T(8,128)(2,1)}), bf16[32,64,256]{2,1,0:T(8,128)(2,1)S(1)}, u32[]{:S(2)}, u32[]{:S(2)}) %all-to-all-start) | async-done | bytes 1048608 | tf_op jit(solution)/shard_map/all_to_all | solution.py:24
  141.5 6.0 %all_to_all.25 = bf16[2,32,64,256]{3,2,1,0:T(8,128)(2,1)S(1)} all-to-all(bf16[2,32,64,256]{3,2,1,0:T(8,128)(2,1)S(1)} %broadcast_in_dim.38), channel_id=1, replica_groups=mesh['groups'=4,'asset_0'=32,'asset_1'=2] {'asset_1'}, dimensions={0} | all-to-all | bytes 4194304 | tf_op jit(solution)/shard_map/all_to_all | solution.py:24
  149.0 23.3 %while.28 = (s32[]{:T(128)}, f32[8,512,128]{2,1,0:T(8,128)S(1)}, f32[1024]{0:T(1024)S(1)}, bf16[8,512,256]{2,1,0:T(8,128)(2,1)}, bf16[1024,256]{1,0:T(8,128)(2,1...) while((s32[]{:T(128)}, f32[8,512,128]{2,1,0:T(8,128)S(1)}, f32[1024]{0:T(1024)S(1)}, ...), condition=%wide.region_1.2_spmd.clone, body=%wide.region_0.1_spmd.clone.sunk | while | flops 410255360 | bytes 1061981 | solution.py:173
  149.0 2.9 fusion.83
  151.9 2.9 fusion.83
  154.8 2.9 fusion.83
  157.7 2.9 fusion.83
  160.6 2.9 fusion.83
  163.6 2.9 fusion.83
  166.5 2.9 fusion.83
  169.4 2.9 fusion.83
  173.6 30.4 %all_to_all.26 = f32[64,1,128]{2,1,0:T(1,128)S(1)} all-to-all(f32[64,1,128]{2,1,0:T(1,128)S(1)} %bitcast.97), channel_id=1, replica_groups=mesh['groups'=4,'asset_0'=32,'asset_1'=2] {'asset_0','asset_1'}, dimensions={0} | all-to-all | bytes 65536 | tf_op jit(solution)/shard_map/all_to_all | solution.py:45
  204.7 6.3 %all-to-all-start.3 = ((f32[64,1,128]{2,1,0:T(1,128)}), f32[64,1,128]{2,1,0:T(1,128)S(1)}, u32[]{:S(2)}, u32[]{:S(2)}) async-start(f32[64,1,128]{2,1,0:T(1,128)} %broadcast_in_dim.39), calls=%async_computation.3 | async-start | bytes 65536 | tf_op jit(solution)/shard_map/all_to_all | solution.py:24
  212.9 20.7 %all-to-all-done.3 = f32[64,1,128]{2,1,0:T(1,128)S(1)} async-done(((f32[64,1,128]{2,1,0:T(1,128)}), f32[64,1,128]{2,1,0:T(1,128)S(1)}, u32[]{:S(2)}, u32[]{:S(2)}) %all-to-all-start.3) | async-done | bytes 32800 | tf_op jit(solution)/shard_map/all_to_all | solution.py:24
  248.5 65.7 %while.29 = (s32[]{:T(128)}, f32[1024,256]{1,0:T(8,128)S(1)}, f32[1024]{0:T(1024)S(1)}, f32[1024]{0:T(1024)S(1)}, bf16[8,512,128]{2,1,0:T(8,128)(2,1)}, /*index=...) while((s32[]{:T(128)}, f32[1024,256]{1,0:T(8,128)S(1)}, ...), condition=%wide.region_18.19_spmd.clone, body=%wide.region_16.18_spmd.clone.sunk | while | flops 681313280 | bytes 15892648 | solution.py:195
  250.0 4.0 fusion.89
  254.0 2.6 convolution_add_fusion.2
  258.2 4.0 fusion.89
  266.4 4.0 fusion.89
  270.4 2.6 convolution_add_fusion.2
  274.7 4.0 fusion.89
  282.9 4.0 fusion.89
  286.9 2.6 convolution_add_fusion.2
  291.1 4.0 fusion.89
  299.3 4.0 fusion.89
  303.3 2.6 convolution_add_fusion.2
  307.5 4.0 fusion.89
  317.7 39.7 %all-reduce = f32[32]{0:T(128)S(1)} all-reduce(f32[32]{0:T(128)S(1)} %dynamic-update-slice), channel_id=1, replica_groups=mesh['groups'=4,'asset_0'=32,'asset_1'=2] {'asset_0'}, use_global_device_ids=true, to_apply=%add | all-reduce | flops 32 | bytes 256
  361.3 16.8 %all-reduce.1 = f32[2]{0:T(128)S(1)} all-reduce(f32[2]{0:T(128)S(1)} %dynamic-update-slice.1), channel_id=1, replica_groups=mesh['groups'=4,'asset_0'=32,'asset_1'=2] {'asset_1'}, use_global_device_ids=true, to_apply=%add.1 | all-reduce | flops 2 | bytes 16
  381.0 38.5 %all-gather.2 = f32[32,1,128]{2,1,0:T(1,128)S(1)} all-gather(f32[1,1,128]{2,1,0:T(1,128)S(1)} %bitcast.99), channel_id=2, replica_groups=mesh['groups'=4,'asset_0'=32,'asset_1'=2] {'asset_0'}, dimensions={0}, use_global_device_ids=true | all-gather | bytes 16896 | tf_op jit(solution)/shard_map/all_gather | solution.py:65
  419.6 16.0 %all-gather.3 = f32[2,1,128]{2,1,0:T(1,128)S(1)} all-gather(f32[1,1,128]{2,1,0:T(1,128)S(1)} %bitcast.100), channel_id=3, replica_groups=mesh['groups'=4,'asset_0'=32,'asset_1'=2] {'asset_1'}, dimensions={0}, use_global_device_ids=true | all-gather | bytes 1536 | tf_op jit(solution)/shard_map/all_gather | solution.py:65
  (100 shorter events, 51.5 us)
Async XLA Ops:
  0.6 0.9 copy-start
  3.5 137.7 %all-to-all-start = ((bf16[32,64,256]{2,1,0:T(8,128)(2,1)}), bf16[32,64,256]{2,1,0:T(8,128)(2,1)S(1)}, u32[]{:S(2)}, u32[]{:S(2)}) async-start(bf16[32,64,256]{2,1,0:T(8,128)(2,1)} %broadcast_in_dim.37), calls=%async_computation | async-start | bytes 2097152 | tf_op jit(solution)/shard_map/all_to_all | solution.py:24
  147.5 1.4 copy-start.2
  147.5 1.4 copy-start.3
  147.5 1.4 copy-start.4
  147.5 1.4 copy-start.7
  149.0 23.4 %copy-start.6 = (f32[128]{0:T(128)S(1)}, f32[128]{0:T(128)}, u32[]{:S(2)}) copy-start(f32[128]{0:T(128)} %param.19) | copy-start | bytes 1540
  172.3 76.2 %copy-start.1 = (f32[8,512,128]{2,1,0:T(8,128)}, f32[8,512,128]{2,1,0:T(8,128)S(1)}, u32[]{:S(2)}) copy-start(f32[8,512,128]{2,1,0:T(8,128)S(1)} %get-tuple-element.206) | copy-start | bytes 6291460
  172.3 38.7 %copy-start.10 = (u32[256]{0:T(256)S(1)}, u32[256]{0:T(256)}, u32[]{:S(2)}) copy-start(u32[256]{0:T(256)} %constant.96) | copy-start | bytes 3076
  172.3 39.3 %copy-start.9 = (u32[256]{0:T(256)S(1)}, u32[256]{0:T(256)}, u32[]{:S(2)}) copy-start(u32[256]{0:T(256)} %constant.101) | copy-start | bytes 3076
  172.3 63.9 %copy-start.5 = (s32[4096]{0:T(1024)S(1)}, s32[4096]{0:T(1024)}, u32[]{:S(2)}) copy-start(s32[4096]{0:T(1024)} %param.18) | copy-start | bytes 49156
  204.7 28.9 %all-to-all-start.3 = ((f32[64,1,128]{2,1,0:T(1,128)}), f32[64,1,128]{2,1,0:T(1,128)S(1)}, u32[]{:S(2)}, u32[]{:S(2)}) async-start(f32[64,1,128]{2,1,0:T(1,128)} %broadcast_in_dim.39), calls=%async_computation.3 | async-start | bytes 65536 | tf_op jit(solution)/shard_map/all_to_all | solution.py:24
  248.5 1.5 copy-start.8
  256.7 1.5 copy-start.8
  264.9 1.5 copy-start.8
  273.1 1.5 copy-start.8
  281.3 1.5 copy-start.8
  289.6 1.5 copy-start.8
  297.8 1.5 copy-start.8
  306.0 1.5 copy-start.8
